TPU v7x, 128 devices: a whole 4x4x4 slice. The times are simulated.
128 devices in a mesh: pi: 8 (over y, x_lo), pj: 16 (over x_hi, z, core).
Axes of the slice: x: 4 (x_hi: 2, x_lo: 2; x = x_hi * 2 + x_lo), y: 4, z: 4, core: 2. Of those that a mesh axis runs over, the one named last changes fastest.
Arguments:
- duo_embedding: bfloat16 [2048, 2048, 128], P('pi', 'pj'), may hold values from -12 to 12
- duo_attention_weights: float32 [128, 8], replicated, may hold values from -16 to 16
- aligned_embedding: bfloat16 [512, 64, 2048], P('pj', None, 'pi'), may hold values from -6 to 6
- aligned_scaling_weights: float32 [64], replicated, may hold values from 0.5 to 1.5
- aligned_shift_vector: float32 [64], replicated, may hold values from -3 to 3
- payload_weights: bfloat16 [64, 256], replicated, may hold values from -0.75 to 0.75
- switch_weights: bfloat16 [64, 256], replicated, may hold values from -0.75 to 0.75
- closing_weights: bfloat16 [256, 64], replicated, may hold values from -1.5 to 1.5
Outputs:
- update: bfloat16 [512, 64, 2048], P('pj', None, 'pi')
All inputs are finite; a program needn't handle non-finite values.
Results may differ from a plain program's by a relative error of at most 0.009.
Values may be sent and summed in bfloat16 or wider, within the bound.
A program may use at most 192 MiB of HBM per device.

v0:
```python
import jax
import jax.numpy as jnp
from jax import lax
from jax.sharding import Mesh
from jax.sharding import PartitionSpec as P

PI = ("pi_0", "pi_1")
EPS = 1e-05


def gathered_total(x, axis):
    return lax.all_gather(x, axis).max(0)


def over_pieces(x, axis):
    blocks = lax.all_gather(x, axis)
    return blocks.sum(axis=0)


def gathered_by_axis(x, axes, dim):
    for axis in reversed(axes):
        x = lax.all_gather(x, axis, axis=dim, tiled=True)
    return x


def rescale_embedding(inputs, axis):
    row_mean = jnp.mean(inputs, axis=axis, keepdims=True)
    centred = inputs - row_mean
    variance = jnp.mean(centred * centred, axis=axis, keepdims=True)
    return centred * lax.rsqrt(variance + EPS)


def body(
    duo_embedding,
    duo_attention_weights,
    aligned_embedding,
    aligned_scaling_weights,
    aligned_shift_vector,
    payload_weights,
    switch_weights,
    closing_weights,
):
    attender_tally = duo_attention_weights.shape[1]
    entry_tally = duo_embedding.shape[0]
    aligned_seq_tally = aligned_embedding.shape[0]
    inner_embed_size = payload_weights.shape[1]
    attender_span = inner_embed_size // attender_tally
    pair_normed = rescale_embedding(duo_embedding.astype(jnp.float32), 2)
    scores = jnp.einsum(
        "ijc,ch->hij", pair_normed, duo_attention_weights, precision=lax.Precision.HIGHEST
    )
    row_peak = gathered_total(jnp.max(scores, axis=2), "pj")
    exp_scores = jnp.exp(scores - row_peak[:, :, None]).astype(jnp.bfloat16)
    row_total = over_pieces(jnp.sum(exp_scores, axis=2, dtype=jnp.float32), "pj")
    weights_full = lax.all_gather(exp_scores, "pj", axis=2, tiled=True)
    rescaled_aligned = (
        rescale_embedding(aligned_embedding.astype(jnp.float32), 1)
        * aligned_scaling_weights[None, :, None]
        + aligned_shift_vector[None, :, None]
    ).astype(jnp.bfloat16)
    switch_share = jax.nn.sigmoid(
        jnp.einsum(
            "scn,ce->sen", rescaled_aligned, switch_weights, preferred_element_type=jnp.float32
        )
    )
    value_segment = jnp.einsum(
        "scn,ce->sen",
        gathered_by_axis(rescaled_aligned, PI, 2),
        payload_weights,
        preferred_element_type=jnp.float32,
    ).astype(jnp.bfloat16)
    piece_span = value_segment.shape[2]
    payload_each_attender = value_segment.reshape(
        aligned_seq_tally, attender_tally, attender_span, piece_span
    )
    numerator = jnp.einsum(
        "hij,shcj->shci", weights_full, payload_each_attender, preferred_element_type=jnp.float32
    )
    gate_per_head = switch_share.reshape(
        aligned_seq_tally, attender_tally, attender_span, entry_tally
    )
    averaged_result = (gate_per_head * (numerator / row_total[None, :, None, :])).astype(
        jnp.bfloat16
    )
    averaged_result = averaged_result.reshape(aligned_seq_tally, inner_embed_size, entry_tally)
    return jnp.einsum(
        "ser,ec->scr", averaged_result, closing_weights, preferred_element_type=jnp.float32
    ).astype(jnp.bfloat16)


def solution(mesh):
    finer = Mesh(mesh.devices.reshape(4, 2, mesh.shape["pj"]), ("pi_0", "pi_1", "pj"))
    placed = (P(PI, "pj", None), P(), P("pj", None, PI), P(), P(), P(), P(), P())
    return jax.shard_map(
        body, mesh=finer, in_specs=placed, out_specs=P("pj", None, PI), check_vma=False
    )
```

profile of v0, /device:TPU:1, one launch (start us, length us, event | category | flops | bytes accessed | tf_op | source)
XLA Modules:
  0.0 258.4 jit_solution(3760978803032783942)
XLA Ops:
  6.5 0.0 copy-start
  6.5 0.0 all-gather.6.cloned.1.call-start
  6.5 1.4 convert_reduce_fusion.1
  8.0 1.6 fusion.17
  9.6 2.7 %fusion.20 = bf16[32,64,256]{2,1,0:T(8,128)(2,1)} fusion(bf16[32,64,256]{2,1,0:T(8,128)(2,1)} %param.10, f32[64]{0:T(128)} %param.12, f32[64]{0:T(128)} %param.11, f32[32,256]{1,0:T(8,128)S(1)} %add_rsqrt_fusion.1, f32[32,256]{1,0:T(8,128)S(1)} %broadcast_multiply_fusion.1), kind=kLoop, calls=%fused_computation.22 | loop fusion | flops 3145728 | bytes 2163200 | tf_op jit(solution)/shard_map/convert_element_type | solution.py:60
  12.3 0.0 all-gather.6.cloned.1.call-update
  12.4 0.0 all-gather.8.cloned.1.call-start
  12.4 38.7 %all-gather.6.cloned.1.call-done = bf16[32,64,512]{2,1,0:T(8,128)(2,1)} async-done(((bf16[32,64,256]{2,1,0:T(8,128)(2,1)}), bf16[32,64,512]{2,1,0:T(8,128)(2,1)}) %all-gather.6.cloned.1.call-update) | async-done | bytes 2097168 | tf_op jit(solution)/shard_map/all_gather | solution.py:22
  51.1 0.0 all-gather.8.cloned.1.call-update
  51.1 0.0 copy-start.5
  51.2 0.0 all-gather.10.cloned.1.call-start
  51.2 0.0 slice-start
  51.2 5.8 %convert_reduce_fusion = f32[256,128]{1,0:T(8,128)S(1)} fusion(bf16[256,128,128]{2,1,0:T(8,128)(2,1)} %param.8), kind=kLoop, calls=%fused_computation.3 | loop fusion | flops 8355840 | bytes 8519680 | tf_op jit(solution)/shard_map/reduce_sum | solution.py:27
  57.0 0.0 slice-start.1
  57.1 10.9 %fusion.4 = f32[256,128]{1,0:T(8,128)S(1)} fusion(bf16[256,128,128]{2,1,0:T(8,128)(2,1)} %param.8, f32[256,128]{1,0:T(8,128)S(1)} %broadcast_multiply_fusion), kind=kLoop, calls=%fused_computation.7 | loop fusion | flops 16744448 | bytes 8650752 | tf_op jit(solution)/shard_map/reduce_sum | solution.py:29
  68.0 0.0 copy-done.5
  68.0 0.0 slice-done
  68.0 0.0 slice-done.1
  68.0 0.0 copy-start.2
  68.0 0.0 copy-start.4
  68.0 31.4 %fusion.29 = (f32[8,256]{0,1:T(8,128)S(1)}, f32[8,256,128]{2,0,1:T(8,128)S(1)}) fusion(f32[128,8]{0,1:T(8,128)S(1)} %copy-done.5, bf16[256,128,128]{2,1,0:T(8,128)(2,1)S(1)} %bitcast.39, f32[256,128]{1,0:T(8,128)S(1)} %add_rsqrt_fusion, f32[256,128]{1,0:T(8,128)S(1)} %broadcast_multiply_fusion), kind=kOutput, calls=%fused_computation.38 | convolution fusion | flops 415496192 | bytes 9711616 | tf_op jit(solution)/shard_map/ijc,ch->hij/dot_general | solution.py:49
  99.4 0.1 copy.26
  99.5 25.0 %all-gather = f32[128,256]{1,0:T(8,128)S(1)} all-gather(f32[8,256]{1,0:T(8,128)S(1)} %copy.26), channel_id=2, replica_groups=mesh['pi_0'=4,'pi_1'=2,'pj'=16] {'pj'}, dimensions={0}, use_global_device_ids=true | all-gather | bytes 139264 | tf_op jit(solution)/shard_map/all_gather | solution.py:12
  124.5 0.1 copy.27
  124.6 1.2 convert_reduce_fusion.2
  125.8 0.0 all-gather.10.cloned.1.call-update
  125.8 0.1 copy.30
  125.9 19.6 %all-gather.1 = f32[128,256]{1,0:T(8,128)S(1)} all-gather(f32[8,256]{1,0:T(8,128)S(1)} %copy.30), channel_id=3, replica_groups=mesh['pi_0'=4,'pi_1'=2,'pj'=16] {'pj'}, dimensions={0}, use_global_device_ids=true | all-gather | bytes 139264 | tf_op jit(solution)/shard_map/all_gather | solution.py:16
  145.5 0.0 copy-done.2
  145.5 0.0 copy-done.4
  145.6 5.9 %add_divide_fusion = f32[32,256,256]{1,2,0:T(8,128)} fusion(bf16[32,64,256]{2,1,0:T(8,128)(2,1)S(1)} %copy-done.2, bf16[64,256]{1,0:T(8,128)(2,1)S(1)} %copy-done.4), kind=kOutput, calls=%fused_computation.14 | convolution fusion | flops 274726912 | bytes 9469952 | tf_op jit(solution)/shard_map/scn,ce->sen/dot_general | solution.py:62
  151.5 0.0 all-gather.8.cloned.1.call-done
  151.5 0.0 copy-done
  151.5 17.4 %convolution_convert_fusion = bf16[32,2048,256]{1,2,0:T(8,128)(2,1)} fusion(bf16[32,64,2048]{2,1,0:T(8,128)(2,1)} %all-gather.8.cloned.1.call-done, bf16[64,256]{1,0:T(8,128)(2,1)S(1)} %copy-done), kind=kOutput, calls=%fused_computation.4 | convolution fusion | flops 2164260864 | bytes 41975808 | tf_op jit(solution)/shard_map/scn,ce->sen/dot_general | solution.py:66
  168.9 48.3 %all-gather.10.cloned.1.call-done = bf16[8,256,2048]{2,0,1:T(8,128)(2,1)} async-done(((bf16[8,256,128]{2,0,1:T(8,128)(2,1)}), bf16[8,256,2048]{2,0,1:T(8,128)(2,1)}) %all-gather.10.cloned.1.call-update) | async-done | bytes 8388624 | tf_op jit(solution)/shard_map/all_gather | solution.py:55
  217.2 0.0 copy-start.1
  217.2 30.2 %fusion.7 = bf16[32,8,32,256]{3,2,0,1:T(8,128)(2,1)} fusion(f32[32,8,32,256]{3,2,1,0:T(8,128)} %bitcast.42, bf16[8,256,2048,1]{2,0,1,3:T(8,128)(2,1)} %bitcast.41, bf16[32,8,32,2048]{3,2,1,0:T(8,128)(2,1)} %bitcast.37, f32[8,256]{1,0:T(8,128)S(1)} %bitcast_reduce_fusion), kind=kOutput, calls=%fused_computation.10 | convolution fusion | flops 8596226048 | bytes 54534144 | tf_op jit(solution)/shard_map/hij,shcj->shci/dot_general | solution.py:76
  247.4 0.0 copy-start.3
  247.4 2.6 %copy.32 = bf16[32,8,32,256]{3,2,1,0:T(8,128)(2,1)S(1)} copy(bf16[32,8,32,256]{3,2,0,1:T(8,128)(2,1)} %fusion.7) | data formatting | bytes 8388608 | tf_op jit(solution)/shard_map/convert_element_type | solution.py:82
  250.1 0.0 copy-done.3
  250.1 1.8 fusion.21
  251.9 0.0 copy-done.1
  (7 shorter events, 0.1 us)
Async XLA Ops:
  6.5 144.9 %copy-start = (bf16[64,256]{1,0:T(8,128)(2,1)S(1)}, bf16[64,256]{1,0:T(8,128)(2,1)}, u32[]{:S(2)}) copy-start(bf16[64,256]{1,0:T(8,128)(2,1)} %param.13) | copy-start | bytes 98308
  6.5 44.6 %all-gather.6.cloned.1.call-start = ((), (), s32[]{:S(2)}) async-start(), calls=%async_computation | async-start | bytes 3145728 | tf_op jit(solution)/shard_map/all_gather | solution.py:22
  12.4 139.1 %all-gather.8.cloned.1.call-start = ((), (), s32[]{:S(2)}) async-start(), calls=%async_computation.1 | async-start | bytes 10485760 | tf_op jit(solution)/shard_map/all_gather | solution.py:22
  51.1 16.8 %copy-start.5 = (f32[128,8]{0,1:T(8,128)S(1)}, f32[128,8]{0,1:T(8,128)}, u32[]{:S(2)}) copy-start(f32[128,8]{0,1:T(8,128)} %param.9) | copy-start | bytes 12292
  51.2 166.1 %all-gather.10.cloned.1.call-start = ((), (), s32[]{:S(2)}) async-start(), calls=%async_computation.2 | async-start | bytes 8912896 | tf_op jit(solution)/shard_map/all_gather | solution.py:55
  51.2 16.8 %slice-start = ((s8[8388608]{0:T(1024)(128)(4,1)}), s8[4194304]{0:T(1024)(128)(4,1)S(1)}, s32[]{:S(2)}) async-start(s8[8388608]{0:T(1024)(128)(4,1)} %bitcast.38), calls=%async_computation.3 | async-start | bytes 8388608
  57.0 10.9 %slice-start.1 = ((s8[8388608]{0:T(1024)(128)(4,1)}), s8[4194304]{0:T(1024)(128)(4,1)S(1)}, s32[]{:S(2)}) async-start(s8[8388608]{0:T(1024)(128)(4,1)} %bitcast.38), calls=%async_computation.4 | async-start | bytes 8388608
  68.0 77.5 %copy-start.2 = (bf16[32,64,256]{2,1,0:T(8,128)(2,1)S(1)}, bf16[32,64,256]{2,1,0:T(8,128)(2,1)}, u32[]{:S(2)}) copy-start(bf16[32,64,256]{2,1,0:T(8,128)(2,1)} %fusion.20) | copy-start | bytes 3145732
  68.0 77.5 %copy-start.4 = (bf16[64,256]{1,0:T(8,128)(2,1)S(1)}, bf16[64,256]{1,0:T(8,128)(2,1)}, u32[]{:S(2)}) copy-start(bf16[64,256]{1,0:T(8,128)(2,1)} %param.14) | copy-start | bytes 98308
  217.2 34.7 %copy-start.1 = (bf16[64,256]{1,0:T(8,128)(2,1)S(1)}, bf16[64,256]{1,0:T(8,128)(2,1)}, u32[]{:S(2)}) copy-start(bf16[64,256]{1,0:T(8,128)(2,1)} %param.13) | copy-start | bytes 98308
  247.4 2.6 %copy-start.3 = (bf16[256,64]{0,1:T(8,128)(2,1)S(1)}, bf16[256,64]{0,1:T(8,128)(2,1)}, u32[]{:S(2)}) copy-start(bf16[256,64]{0,1:T(8,128)(2,1)} %param.15) | copy-start | bytes 98308
Sparse Core Ops, SparseCore 0:
  12.5 38.5 all-gather.5
  52.8 84.0 all-gather.7
  139.2 78.0 all-gather.9
where the time goes:
time: 259 us; the launch traced here: 258 us
  waiting for transfers between devices  87.1 us (34%)
  matrix products  86.8 us (34%)
  blocking collectives  44.6 us (17%)
  other arithmetic  23.7 us (9%)
  between operations  13.3 us (5%)
  local copies, waits for them, and re-layouts  2.92 us (1%)
    all_gather x1, waiting for transfers between devices, body(): weights_full = lax.all_gather(exp_scores, 'pj', axis=2, tiled=True)  48.3 us
    all_gather x2, waiting for transfers between devices, gathered_by_axis(): x = lax.all_gather(x, axis, axis=dim, tiled=True)  38.7 us
    dot_general x1, matrix products, body(): jnp.einsum('ijc,ch->hij', pair_normed, duo_attention_weights, precision=l...  31.4 us
    dot_general x1, matrix products, body(): jnp.einsum('hij,shcj->shci', weights_full, payload_each_attender, preferr...  30.2 us
    all_gather x1, blocking collectives, gathered_total(): return lax.all_gather(x, axis).max(0)  25 us
    all_gather x1, blocking collectives, over_pieces(): blocks = lax.all_gather(x, axis)  19.6 us
    dot_general x1, matrix products, body(): jnp.einsum('scn,ce->sen', gathered_by_axis(rescaled_aligned, PI, 2), payl...  17.4 us
    reduce_sum x2, other arithmetic, rescale_embedding(): variance = jnp.mean(centred * centred, axis=axis, keepdims=True)  12.5 us
  transfers between devices with their start and end apart: 3, of which 2 were waited for; matrix products, arithmetic and copies ran while one was open for 28% of the time, Pallas kernels for 0%

commit v1 on v0

--- a/solution.py
+++ b/solution.py
@@ -6,6 +6,14 @@
 
 PI = ("pi_0", "pi_1")
 EPS = 1e-05
+
+
+def region_enter(values):
+    left_arr = jnp.concatenate(
+        jax.lax.all_to_all(jnp.stack(jax.lax.axis_size("pj") * [values], axis=0), "pj", 0, 0),
+        axis=2,
+    )
+    return left_arr
 
 
 def gathered_total(x, axis):
@@ -52,7 +60,7 @@
     row_peak = gathered_total(jnp.max(scores, axis=2), "pj")
     exp_scores = jnp.exp(scores - row_peak[:, :, None]).astype(jnp.bfloat16)
     row_total = over_pieces(jnp.sum(exp_scores, axis=2, dtype=jnp.float32), "pj")
-    weights_full = lax.all_gather(exp_scores, "pj", axis=2, tiled=True)
+    weights_full = region_enter(exp_scores)
     rescaled_aligned = (
         rescale_embedding(aligned_embedding.astype(jnp.float32), 1)
         * aligned_scaling_weights[None, :, None]

time: 259 us -> 356 us (1.37)
  blocking collectives: 44.6 us -> 165 us
  waiting for transfers between devices: 87.1 us -> 38.7 us
  local copies, waits for them, and re-layouts: 2.92 us -> 33.6 us
  matrix products: 86.8 us -> 76.5 us
  starting transfers between devices: 0.08 us -> 4.83 us
    all_gather x1, blocking collectives: 19.6 us -> 140 us  [over_pieces(): blocks = lax.all_gather(x, axis)]
    all_gather x1 -> x0, waiting for transfers between devices: 48.3 us -> none  [body(): weights_full = lax.all_gather(exp_scores, 'pj', axis=2, tiled=True)]
    reshape x0 -> x2, local copies, waits for them, and re-layouts: none -> 25.3 us  [region_enter(): jnp.concatenate(jax.lax.all_to_all(jnp.stack(jax.lax.axis_size('pj') * [v...]
    dot_general x1, matrix products: 30.2 us -> 20.1 us  [body(): jnp.einsum('hij,shcj->shci', weights_full, payload_each_attender, preferr...]
    another operation x0 -> x1, local copies, waits for them, and re-layouts: none -> 5.3 us  [region_enter(): jnp.stack(jax.lax.axis_size('pj') * [values], axis=0)]
    all_to_all x0 -> x1, starting transfers between devices: none -> 4.79 us  [region_enter(): jax.lax.all_to_all(jnp.stack(jax.lax.axis_size('pj') * [values], axis=0),...]
  transfers between devices with their start and end apart: 3 -> 3, of which waited for: 2 -> 1; matrix products, arithmetic and copies ran while one was open for 28% -> 24% of each run, Pallas kernels for 0% -> 0%
where the time goes in v1:
time: 356 us; the launch traced here: 355 us
  blocking collectives  165 us (46%)
  matrix products  76.5 us (21%)
  waiting for transfers between devices  38.7 us (11%)
  local copies, waits for them, and re-layouts  33.6 us (9%)
  other arithmetic  23.1 us (6%)
  between operations  13.6 us (4%)
  starting transfers between devices  4.83 us (1%)
    all_gather x1, blocking collectives, over_pieces(): blocks = lax.all_gather(x, axis)  140 us
    all_gather x2, waiting for transfers between devices, gathered_by_axis(): x = lax.all_gather(x, axis, axis=dim, tiled=True)  38.7 us
    dot_general x1, matrix products, body(): jnp.einsum('ijc,ch->hij', pair_normed, duo_attention_weights, precision=l...  31.4 us
    reshape x2, local copies, waits for them, and re-layouts, region_enter(): jnp.concatenate(jax.lax.all_to_all(jnp.stack(jax.lax.axis_size('pj') * [v...  25.3 us
    all_gather x1, blocking collectives, gathered_total(): return lax.all_gather(x, axis).max(0)  25 us
    dot_general x1, matrix products, body(): jnp.einsum('hij,shcj->shci', weights_full, payload_each_attender, preferr...  20.1 us
    dot_general x1, matrix products, body(): jnp.einsum('scn,ce->sen', gathered_by_axis(rescaled_aligned, PI, 2), payl...  17.3 us
    reduce_sum x2, other arithmetic, rescale_embedding(): variance = jnp.mean(centred * centred, axis=axis, keepdims=True)  12.5 us
  transfers between devices with their start and end apart: 3, of which 1 were waited for; matrix products, arithmetic and copies ran while one was open for 24% of the time, Pallas kernels for 0%

profile of v1, /device:TPU:1, one launch (start us, length us, event | category | flops | bytes accessed | tf_op | source)
XLA Modules:
  0.0 355.4 jit_solution(1562562548273707315)
XLA Ops:
  6.5 0.0 copy-start
  6.5 0.0 all-gather.5.cloned.1.call-start
  6.5 1.4 convert_reduce_fusion.1
  8.0 1.6 fusion.17
  9.6 2.7 fusion.20
  12.3 0.0 all-gather.5.cloned.1.call-update
  12.4 0.0 all-gather.7.cloned.1.call-start
  12.4 38.7 %all-gather.5.cloned.1.call-done = bf16[32,64,512]{2,1,0:T(8,128)(2,1)} async-done(((bf16[32,64,256]{2,1,0:T(8,128)(2,1)}), bf16[32,64,512]{2,1,0:T(8,128)(2,1)}) %all-gather.5.cloned.1.call-update) | async-done | bytes 2097168 | tf_op jit(solution)/shard_map/all_gather | solution.py:30
  51.1 0.0 all-gather.7.cloned.1.call-update
  51.1 0.0 slice-start
  51.2 0.0 copy-start.5
  51.2 5.8 %convert_reduce_fusion = f32[256,128]{1,0:T(8,128)S(1)} fusion(bf16[256,128,128]{2,1,0:T(8,128)(2,1)} %param.8), kind=kLoop, calls=%fused_computation.3 | loop fusion | flops 8355840 | bytes 8519680 | tf_op jit(solution)/shard_map/reduce_sum | solution.py:35
  57.0 0.0 slice-start.1
  57.0 10.9 %fusion.4 = f32[256,128]{1,0:T(8,128)S(1)} fusion(bf16[256,128,128]{2,1,0:T(8,128)(2,1)} %param.8, f32[256,128]{1,0:T(8,128)S(1)} %broadcast_multiply_fusion), kind=kLoop, calls=%fused_computation.7 | loop fusion | flops 16744448 | bytes 8650752 | tf_op jit(solution)/shard_map/reduce_sum | solution.py:37
  67.9 0.0 slice-done
  67.9 0.0 copy-done.5
  67.9 0.0 slice-done.1
  67.9 31.4 %fusion.29 = (f32[8,256]{0,1:T(8,128)S(1)}, f32[8,256,128]{2,0,1:T(8,128)S(1)}) fusion(f32[128,8]{0,1:T(8,128)S(1)} %copy-done.5, bf16[256,128,128]{2,1,0:T(8,128)(2,1)S(1)} %bitcast.46, f32[256,128]{1,0:T(8,128)S(1)} %add_rsqrt_fusion, f32[256,128]{1,0:T(8,128)S(1)} %broadcast_multiply_fusion), kind=kOutput, calls=%fused_computation.38 | convolution fusion | flops 415496192 | bytes 9711616 | tf_op jit(solution)/shard_map/ijc,ch->hij/dot_general | solution.py:57
  99.4 0.1 copy.28
  99.4 25.0 %all-gather = f32[128,256]{1,0:T(8,128)S(1)} all-gather(f32[8,256]{1,0:T(8,128)S(1)} %copy.28), channel_id=2, replica_groups=mesh['pi_0'=4,'pi_1'=2,'pj'=16] {'pj'}, dimensions={0}, use_global_device_ids=true | all-gather | bytes 139264 | tf_op jit(solution)/shard_map/all_gather | solution.py:20
  124.4 0.1 copy.29
  124.6 0.6 convert_reduce_fusion.2
  125.2 0.1 copy.30
  125.3 5.3 %stack.2 = bf16[16,8,256,128]{3,2,1,0:T(8,128)(2,1)} broadcast(bf16[8,256,128]{2,1,0:T(8,128)(2,1)S(1)} %copy.30), dimensions={1,2,3} | broadcast | bytes 8912896 | tf_op jit(solution)/shard_map/stack | solution.py:13
  130.6 0.0 copy-start.2
  130.6 0.0 copy-start.4
  130.6 4.8 %all-to-all-start = ((bf16[16,8,256,128]{3,2,1,0:T(8,128)(2,1)}), bf16[16,8,256,128]{3,2,1,0:T(8,128)(2,1)}, u32[]{:S(2)}, u32[]{:S(2)}) async-start(bf16[16,8,256,128]{3,2,1,0:T(8,128)(2,1)} %stack.2), calls=%async_computation | async-start | bytes 16777216 | tf_op jit(solution)/shard_map/all_to_all | solution.py:13
  135.4 0.1 copy.33
  135.5 140.0 %all-gather.1 = f32[128,256]{1,0:T(8,128)S(1)} all-gather(f32[8,256]{1,0:T(8,128)S(1)} %copy.33), channel_id=3, replica_groups=mesh['pi_0'=4,'pi_1'=2,'pj'=16] {'pj'}, dimensions={0}, use_global_device_ids=true | all-gather | bytes 139264 | tf_op jit(solution)/shard_map/all_gather | solution.py:24
  275.5 0.0 copy-done.2
  275.5 0.0 copy-done.4
  275.5 5.9 %add_divide_fusion = f32[32,256,256]{1,2,0:T(8,128)} fusion(bf16[32,64,256]{2,1,0:T(8,128)(2,1)S(1)} %copy-done.2, bf16[64,256]{1,0:T(8,128)(2,1)S(1)} %copy-done.4), kind=kOutput, calls=%fused_computation.14 | convolution fusion | flops 274726912 | bytes 9469952 | tf_op jit(solution)/shard_map/scn,ce->sen/dot_general | solution.py:70
  281.4 0.0 all-to-all-done
  281.4 12.0 %copy.31 = bf16[8,256,16,128]{3,2,1,0:T(8,128)(2,1)} copy(bf16[8,256,16,128]{3,1,0,2:T(8,128)(2,1)} %bitcast.9) | data formatting | bytes 16777216 | tf_op jit(solution)/shard_map/reshape | solution.py:12
  293.4 13.3 %reshape.55 = bf16[8,256,2048,1]{2,1,0,3:T(8,128)(2,1)} reshape(bf16[8,256,16,128]{3,2,1,0:T(8,128)(2,1)} %copy.31) | data formatting | bytes 16777216 | tf_op jit(solution)/shard_map/reshape | solution.py:12
  306.7 0.0 all-gather.7.cloned.1.call-done
  306.7 0.0 copy-done
  306.7 17.3 %convolution_convert_fusion = bf16[32,2048,256]{1,2,0:T(8,128)(2,1)} fusion(bf16[32,64,2048]{2,1,0:T(8,128)(2,1)} %all-gather.7.cloned.1.call-done, bf16[64,256]{1,0:T(8,128)(2,1)S(1)} %copy-done), kind=kOutput, calls=%fused_computation.4 | convolution fusion | flops 2164260864 | bytes 41975808 | tf_op jit(solution)/shard_map/scn,ce->sen/dot_general | solution.py:74
  324.0 0.0 copy-start.1
  324.0 20.1 %fusion.7 = bf16[32,8,32,256]{3,2,0,1:T(8,128)(2,1)} fusion(f32[32,8,32,256]{3,2,1,0:T(8,128)} %bitcast.48, bf16[8,256,2048,1]{2,1,0,3:T(8,128)(2,1)} %reshape.55, bf16[32,8,32,2048]{3,2,1,0:T(8,128)(2,1)} %bitcast.44, f32[8,256]{1,0:T(8,128)S(1)} %bitcast_reduce_fusion), kind=kOutput, calls=%fused_computation.10 | convolution fusion | flops 8596226048 | bytes 54534144 | tf_op jit(solution)/shard_map/hij,shcj->shci/dot_general | solution.py:84
  344.1 0.0 copy-start.3
  344.1 2.6 copy.35
  346.7 0.0 copy-done.3
  346.8 1.8 fusion.21
  348.6 0.0 copy-done.1
  (7 shorter events, 0.1 us)
Async XLA Ops:
  6.5 300.2 %copy-start = (bf16[64,256]{1,0:T(8,128)(2,1)S(1)}, bf16[64,256]{1,0:T(8,128)(2,1)}, u32[]{:S(2)}) copy-start(bf16[64,256]{1,0:T(8,128)(2,1)} %param.13) | copy-start | bytes 98308
  6.5 44.6 %all-gather.5.cloned.1.call-start = ((), (), s32[]{:S(2)}) async-start(), calls=%async_computation.1 | async-start | bytes 3145728 | tf_op jit(solution)/shard_map/all_gather | solution.py:30
  12.4 294.3 %all-gather.7.cloned.1.call-start = ((), (), s32[]{:S(2)}) async-start(), calls=%async_computation.2 | async-start | bytes 10485760 | tf_op jit(solution)/shard_map/all_gather | solution.py:30
  51.1 16.8 %slice-start = ((s8[8388608]{0:T(1024)(128)(4,1)}), s8[4194304]{0:T(1024)(128)(4,1)S(1)}, s32[]{:S(2)}) async-start(s8[8388608]{0:T(1024)(128)(4,1)} %bitcast.45), calls=%async_computation.3 | async-start | bytes 8388608
  51.2 16.8 %copy-start.5 = (f32[128,8]{0,1:T(8,128)S(1)}, f32[128,8]{0,1:T(8,128)}, u32[]{:S(2)}) copy-start(f32[128,8]{0,1:T(8,128)} %param.9) | copy-start | bytes 12292
  57.0 10.9 %slice-start.1 = ((s8[8388608]{0:T(1024)(128)(4,1)}), s8[4194304]{0:T(1024)(128)(4,1)S(1)}, s32[]{:S(2)}) async-start(s8[8388608]{0:T(1024)(128)(4,1)} %bitcast.45), calls=%async_computation.4 | async-start | bytes 8388608
  130.6 144.9 %copy-start.2 = (bf16[32,64,256]{2,1,0:T(8,128)(2,1)S(1)}, bf16[32,64,256]{2,1,0:T(8,128)(2,1)}, u32[]{:S(2)}) copy-start(bf16[32,64,256]{2,1,0:T(8,128)(2,1)} %fusion.20) | copy-start | bytes 3145732
  130.6 144.9 %copy-start.4 = (bf16[64,256]{1,0:T(8,128)(2,1)S(1)}, bf16[64,256]{1,0:T(8,128)(2,1)}, u32[]{:S(2)}) copy-start(bf16[64,256]{1,0:T(8,128)(2,1)} %param.14) | copy-start | bytes 98308
  130.6 150.8 %all-to-all-start = ((bf16[16,8,256,128]{3,2,1,0:T(8,128)(2,1)}), bf16[16,8,256,128]{3,2,1,0:T(8,128)(2,1)}, u32[]{:S(2)}, u32[]{:S(2)}) async-start(bf16[16,8,256,128]{3,2,1,0:T(8,128)(2,1)} %stack.2), calls=%async_computation | async-start | bytes 16777216 | tf_op jit(solution)/shard_map/all_to_all | solution.py:13
  324.0 24.6 %copy-start.1 = (bf16[64,256]{1,0:T(8,128)(2,1)S(1)}, bf16[64,256]{1,0:T(8,128)(2,1)}, u32[]{:S(2)}) copy-start(bf16[64,256]{1,0:T(8,128)(2,1)} %param.13) | copy-start | bytes 98308
  344.1 2.6 copy-start.3
Sparse Core Ops, SparseCore 0:
  12.5 38.5 all-gather.4
  52.8 84.0 all-gather.6
